TPU v7x, 512 devices: a whole 4x4x16 slice. The times are simulated.
512 devices in a mesh: group: 8 (over x, y_hi), vocab: 64 (over z, y_lo, core).
Axes of the slice: x: 4, y: 4 (y_hi: 2, y_lo: 2; y = y_hi * 2 + y_lo), z: 16, core: 2. Of those that a mesh axis runs over, the one named last changes fastest.
Arguments:
- table: bfloat16 [4608, 196608], P('vocab', 'group')
- hidden: bfloat16 [448, 4608], P(None, 'vocab')
- gain: bfloat16 [4608], P('vocab'), may hold values from 0.099609375 to 1.8984375
- ids: int32 [448], replicated, may hold values from 0 to 196607
Outputs:
- next_embed: bfloat16 [448, 4608], P(None, 'vocab')
- logprobs: float32 [448, 196608], P(None, ('group', 'vocab'))
- chosen: float32 [448], replicated
All inputs are finite; a program needn't handle non-finite values.
Results may differ from a plain program's by a relative error of at most 0.001.
Values may be sent and summed in bfloat16 or wider, within the bound.
No kernel may reach another device: no remote copies, remote signals or barrier semaphores. Data moves between devices by JAX's collectives and lax.ppermute only.
A program may use at most 64 MiB of HBM per device.

v0:
```python
import math
import jax
import jax.numpy as jnp
from jax import lax
from jax.sharding import Mesh
from jax.sharding import PartitionSpec as P

VOCAB = ("vocab_0", "vocab_1", "vocab_2")
GROUP = ("group_0", "group_1")
GROUP_VOCAB = ("group_0", "group_1", "vocab_0", "vocab_1", "vocab_2")


def gather_turned(arrays, axis, dims):
    turned = [jnp.moveaxis(a, dim, 0) for a, dim in zip(arrays, dims)]
    both = jnp.concatenate([t.reshape(len(t), -1) for t in turned], axis=1)
    out, at, done = (lax.all_gather(both, axis, axis=0, tiled=True), 0, [])
    for t, dim in zip(turned, dims):
        slab = out[:, at : at + t[0].size].reshape(-1, *t.shape[1:])
        done.append(jnp.moveaxis(slab, 0, dim))
        at += t[0].size
    return tuple(done)


def in_blocks(array, dim, size):
    before, after = (array.shape[:dim], array.shape[dim + 1 :])
    return jnp.moveaxis(array.reshape(*before, size, -1, *after), dim, 0)


def cut_rows(length, count):
    lap = length // count
    if lap >= 8:
        lap -= lap % 8
    return [lap * k for k in range(1, count)]


def in_order(blocks, dim):
    lengths = list(blocks.shape[1:])
    lengths[dim] *= blocks.shape[0]
    return jnp.moveaxis(blocks, 0, dim).reshape(lengths)


def several_exchanges(array, axis, pieces, split_dim, concat_dim):
    blocks = in_blocks(array, split_dim, lax.axis_size(axis))
    widest = max(range(1, max(2, blocks.ndim - 1)), key=lambda d: blocks.shape[d])
    done = []
    for slab in jnp.split(blocks, cut_rows(blocks.shape[widest], pieces), axis=widest):
        if slab.size:
            done.append(lax.all_to_all(slab, axis, split_axis=0, concat_axis=0, tiled=True))
    return in_order(jnp.concatenate(done, axis=widest), concat_dim)


def over_axes(array, axes):
    for axis in axes:
        array = lax.psum(array, axis)
    return array


def body(table, hidden, gain, ids):
    share, span_cols = table.shape
    groups_n = lax.axis_size(VOCAB)
    voc_cols = span_cols // groups_n
    width = share * groups_n
    group_index = lax.axis_index(GROUP)
    vocab_index = lax.axis_index(VOCAB)
    local_ids = ids - group_index * span_cols
    inside = jnp.logical_and(local_ids >= 0, local_ids < span_cols)
    found = jnp.take(table, jnp.clip(local_ids, 0, span_cols - 1), axis=1).astype(jnp.float32).T
    found = found * inside[:, None].astype(jnp.float32)
    embed_cols = lax.psum(found.astype(jnp.bfloat16), GROUP).astype(jnp.float32)
    next_embed = (embed_cols * math.sqrt(width)).astype(jnp.bfloat16)
    whole, gain_all = gather_turned((hidden, gain), VOCAB, (1, 0))
    states = whole.astype(jnp.float32)
    mean_sq = jnp.sum(states * states, axis=1, keepdims=True) / width
    normed = (states * gain_all.astype(jnp.float32) * lax.rsqrt(mean_sq + 1e-06)).astype(
        jnp.bfloat16
    )
    full_cols = several_exchanges(table, VOCAB, 2, 1, 0)
    logits = jnp.dot(normed, full_cols, preferred_element_type=jnp.float32)
    capped = 30.0 * jnp.tanh(logits / 30.0)
    first_col = (group_index * groups_n + vocab_index) * voc_cols
    offsets = ids - first_col
    columns = lax.broadcasted_iota(jnp.int32, capped.shape, 1)
    pick = jnp.sum(jnp.where(columns == offsets[:, None], capped, 0.0), axis=1)
    sums, picks = (
        over_axes(jnp.sum(jnp.exp(capped), axis=1), GROUP_VOCAB),
        over_axes(pick, GROUP_VOCAB),
    )
    log_total = jnp.log(sums)
    logprobs = capped - log_total[:, None]
    chosen = picks - log_total
    return (next_embed, logprobs, chosen)


def solution(mesh):
    torus = Mesh(
        mesh.devices.reshape(4, 2, 16, 2, 2),
        ("group_0", "group_1", "vocab_0", "vocab_1", "vocab_2"),
    )
    return jax.shard_map(
        body,
        mesh=torus,
        in_specs=(P(VOCAB, GROUP), P(None, VOCAB), P(VOCAB), P()),
        out_specs=(P(None, VOCAB), P(None, GROUP_VOCAB), P()),
        check_vma=False,
    )
```

profile of v0, /device:TPU:1, one launch (start us, length us, event | category | flops | bytes accessed | tf_op | source)
XLA Modules:
  0.0 301.4 jit_solution(11320559064461386992)
XLA Ops:
  7.2 2.8 copy.22
  9.9 0.0 copy-start.3
  9.9 0.2 split.8
  10.1 2.1 copy.19
  12.2 18.3 %all-to-all-start = ((bf16[64,32,384]{2,1,0:T(8,128)(2,1)}), bf16[64,32,384]{2,1,0:T(8,128)(2,1)}, u32[]{:S(2)}, u32[]{:S(2)}) async-start(bf16[64,32,384]{2,1,0:T(8,128)(2,1)} %copy.19), calls=%async_computation | async-start | bytes 3145728 | tf_op jit(solution)/shard_map/all_to_all | solution.py:48
  30.5 0.0 all-gather.2.cloned.1.call-start
  30.5 0.0 copy-done.3
  30.6 0.7 copy.18
  31.3 1.6 pad_maximum_fusion.1
  32.9 0.0 all-gather.2.cloned.1.call-update
  32.9 0.2 split.9
  33.1 0.0 copy-start
  33.1 2.4 copy.20
  35.6 79.7 %all-to-all-done = bf16[64,32,384]{2,1,0:T(8,128)(2,1)} async-done(((bf16[64,32,384]{2,1,0:T(8,128)(2,1)}), bf16[64,32,384]{2,1,0:T(8,128)(2,1)}, u32[]{:S(2)}, u32[]{:S(2)}) %all-to-all-start) | async-done | bytes 1572896 | tf_op jit(solution)/shard_map/all_to_all | solution.py:48
  115.3 6.8 %all-to-all-start.1 = ((bf16[64,40,384]{2,1,0:T(8,128)(2,1)}), bf16[64,40,384]{2,1,0:T(8,128)(2,1)}, u32[]{:S(2)}, u32[]{:S(2)}) async-start(bf16[64,40,384]{2,1,0:T(8,128)(2,1)} %copy.20), calls=%async_computation.1 | async-start | bytes 3932160 | tf_op jit(solution)/shard_map/all_to_all | solution.py:48
  122.1 0.0 copy-done
  122.1 0.0 copy-start.2
  122.1 5.3 %copy.17 = bf16[72,24576]{0,1:T(8,128)(2,1)} copy(bf16[72,24576]{1,0:T(8,128)(2,1)S(1)} %copy-done) | data formatting | bytes 7077888 | tf_op args[0]
  127.4 0.0 copy-done.2
  127.4 4.8 %gather_fusion = bf16[448,72]{1,0:T(8,128)(2,1)S(1)} fusion(bf16[72,24576]{0,1:T(8,128)(2,1)} %copy.17, s32[1024]{0:T(1024)S(1)} %pad_clamp_fusion), kind=kCustom, calls=%fused_computation | custom fusion | bytes 130816 | tf_op jit(solution)/shard_map/jit(_take)/gather | solution.py:67
  132.2 0.2 multiply_convert_fusion
  132.4 38.7 %psum.77 = bf16[448,72]{1,0:T(8,128)(2,1)S(1)} all-reduce(bf16[448,72]{1,0:T(8,128)(2,1)S(1)} %multiply_convert_fusion), channel_id=1, replica_groups=mesh['group_0'=4,'group_1'=2,'vocab_0'=16,'vocab_1'=2,'vocab_2'=2] {'gro..., use_global_device_ids=true, to_apply=%region_0.1 | all-reduce | flops 32256 | bytes 129024 | tf_op jit(solution)/shard_map/psum | solution.py:69
  171.1 0.7 copy.21
  171.9 55.3 %all-to-all-done.1 = bf16[64,40,384]{2,1,0:T(8,128)(2,1)} async-done(((bf16[64,40,384]{2,1,0:T(8,128)(2,1)}), bf16[64,40,384]{2,1,0:T(8,128)(2,1)}, u32[]{:S(2)}, u32[]{:S(2)}) %all-to-all-start.1) | async-done | bytes 1966112 | tf_op jit(solution)/shard_map/all_to_all | solution.py:48
  227.1 2.4 pad_maximum_fusion
  229.5 0.0 all-gather.2.cloned.1.call-done
  229.5 0.0 copy-start.1
  229.5 3.6 %fusion.2 = f32[448]{0:T(512)S(1)} fusion(bf16[4608,449]{1,0:T(8,128)(2,1)} %all-gather.2.cloned.1.call-done), kind=kLoop, calls=%fused_computation.5 | loop fusion | flops 6192704 | bytes 4130560 | tf_op jit(solution)/shard_map/reduce_sum | solution.py:73
  233.1 0.2 copy-done.1
  233.3 0.8 convert_reduce_fusion
  234.1 4.3 %select_reduce_fusion = (f32[448]{0:T(512)S(1)}, f32[448]{0:T(512)S(1)}, f32[448,384]{1,0:T(8,128)}) fusion(s32[448]{0:T(512)S(1)} %broadcast_subtract_fusion.1, bf16[4608,384]{1,0:T(8,128)(2,1)S(1)} %bitcast.11, f32[448]{0:T(512)S(1)} %add_rsqrt_fusion, f32[4608]{0:T(1024)S(1)} %convert_reduce_fusion, bf16[4608,449]{1,0:T(8,128)(2,1)S(1)} %copy-done.1), kind=kOutput, calls=%fused_computation.15 | convolution fusion | flops 1594735616 | bytes 8390656 | tf_op jit(solution)/shard_map/dot_general | solution.py:78
  238.4 8.3 %all-reduce.1 = (f32[448]{0:T(512)S(1)}, f32[448]{0:T(512)S(1)}) all-reduce(f32[448]{0:T(512)S(1)} %get-tuple-element.16, f32[448]{0:T(512)S(1)} %get-tuple-element.15), channel_id=1, replica_groups=mesh['group_0'=4,'group_1'=2,'vocab_0'=16,'vocab_1'=2,'vocab_2'=2] {'gro..., use_global_device_ids=true, to_apply=%region_3.4 | all-reduce | flops 896 | bytes 7168 | tf_op jit(solution)/shard_map/psum | solution.py:54
  246.8 5.5 %all-reduce.4 = (f32[448]{0:T(512)S(1)}, f32[448]{0:T(512)S(1)}) all-reduce(f32[448]{0:T(512)S(1)} %get-tuple-element.19, f32[448]{0:T(512)S(1)} %get-tuple-element.20), channel_id=1, replica_groups=mesh['group_0'=4,'group_1'=2,'vocab_0'=16,'vocab_1'=2,'vocab_2'=2] {'gro..., use_global_device_ids=true, to_apply=%region_4.5 | all-reduce | flops 896 | bytes 7168 | tf_op jit(solution)/shard_map/psum | solution.py:54
  252.3 22.0 %all-reduce = (f32[448]{0:T(512)S(1)}, f32[448]{0:T(512)S(1)}) all-reduce(f32[448]{0:T(512)S(1)} %get-tuple-element.25, f32[448]{0:T(512)S(1)} %get-tuple-element.26), channel_id=1, replica_groups=mesh['group_0'=4,'group_1'=2,'vocab_0'=16,'vocab_1'=2,'vocab_2'=2] {'voc..., use_global_device_ids=true, to_apply=%region_5.6 | all-reduce | flops 896 | bytes 7168 | tf_op jit(solution)/shard_map/psum | solution.py:54
  274.3 3.8 %all-reduce.3 = (f32[448]{0:T(512)S(1)}, f32[448]{0:T(512)S(1)}) all-reduce(f32[448]{0:T(512)S(1)} %get-tuple-element.17, f32[448]{0:T(512)S(1)} %get-tuple-element.18), channel_id=1, replica_groups=mesh['group_0'=4,'group_1'=2,'vocab_0'=16,'vocab_1'=2,'vocab_2'=2] {'voc..., use_global_device_ids=true, to_apply=%region_6.7 | all-reduce | flops 896 | bytes 7168 | tf_op jit(solution)/shard_map/psum | solution.py:54
  278.1 13.8 %all-reduce.2 = (f32[448]{0:T(512)S(1)}, f32[448]{0:T(512)S(1)}) all-reduce(f32[448]{0:T(512)S(1)} %get-tuple-element.23, f32[448]{0:T(512)S(1)} %get-tuple-element.24), channel_id=1, replica_groups=mesh['group_0'=4,'group_1'=2,'vocab_0'=16,'vocab_1'=2,'vocab_2'=2] {'voc..., use_global_device_ids=true, to_apply=%region_7.8 | all-reduce | flops 896 | bytes 7168 | tf_op jit(solution)/shard_map/psum | solution.py:54
  291.9 0.6 log_subtract_fusion
  292.5 2.1 broadcast_subtract_fusion
  (5 shorter events, 0.1 us)
Async XLA Ops:
  9.9 20.6 %copy-start.3 = (bf16[72]{0:T(256)(128)(2,1)S(1)}, bf16[72]{0:T(256)(128)(2,1)}, u32[]{:S(2)}) copy-start(bf16[72]{0:T(256)(128)(2,1)} %param.6) | copy-start | bytes 436
  12.2 103.1 %all-to-all-start = ((bf16[64,32,384]{2,1,0:T(8,128)(2,1)}), bf16[64,32,384]{2,1,0:T(8,128)(2,1)}, u32[]{:S(2)}, u32[]{:S(2)}) async-start(bf16[64,32,384]{2,1,0:T(8,128)(2,1)} %copy.19), calls=%async_computation | async-start | bytes 3145728 | tf_op jit(solution)/shard_map/all_to_all | solution.py:48
  30.5 199.0 %all-gather.2.cloned.1.call-start = ((), (), s32[]{:S(2)}) async-start(), calls=%async_computation.2 | async-start | bytes 4792320 | tf_op jit(solution)/shard_map/all_gather | solution.py:16
  33.1 89.0 %copy-start = (bf16[72,24576]{1,0:T(8,128)(2,1)S(1)}, bf16[72,24576]{1,0:T(8,128)(2,1)}, u32[]{:S(2)}) copy-start(bf16[72,24576]{1,0:T(8,128)(2,1)} %param.4) | copy-start | bytes 10616836
  115.3 111.9 %all-to-all-start.1 = ((bf16[64,40,384]{2,1,0:T(8,128)(2,1)}), bf16[64,40,384]{2,1,0:T(8,128)(2,1)}, u32[]{:S(2)}, u32[]{:S(2)}) async-start(bf16[64,40,384]{2,1,0:T(8,128)(2,1)} %copy.20), calls=%async_computation.1 | async-start | bytes 3932160 | tf_op jit(solution)/shard_map/all_to_all | solution.py:48
  122.1 5.3 %copy-start.2 = (s32[448]{0:T(512)S(1)}, s32[448]{0:T(512)}, u32[]{:S(2)}) copy-start(s32[448]{0:T(512)} %param.7) | copy-start | bytes 5380
  229.5 3.8 %copy-start.1 = (bf16[4608,449]{1,0:T(8,128)(2,1)S(1)}, bf16[4608,449]{1,0:T(8,128)(2,1)}, u32[]{:S(2)}) copy-start(bf16[4608,449]{1,0:T(8,128)(2,1)} %all-gather.2.cloned.1.call-done) | copy-start | bytes 12413956
Sparse Core Ops, SparseCore 0:
  34.0 191.4 all-gather.1
where the time goes:
time: 302 us; the launch traced here: 301 us
  waiting for transfers between devices  135 us (45%)
  blocking collectives  92.1 us (30%)
  starting transfers between devices  25.2 us (8%)
  local copies, waits for them, and re-layouts  19.4 us (6%)
  between operations  14.2 us (5%)
  other arithmetic  11.3 us (4%)
  matrix products  4.32 us (1%)
    all_to_all x2, waiting for transfers between devices, several_exchanges(): lax.all_to_all(slab, axis, split_axis=0, concat_axis=0, tiled=True)  135 us
    psum x5, blocking collectives, over_axes(): array = lax.psum(array, axis)  53.4 us
    psum x1, blocking collectives, body(): embed_cols = lax.psum(found.astype(jnp.bfloat16), GROUP).astype(jnp.float32)  38.7 us
    all_to_all x2, starting transfers between devices, several_exchanges(): lax.all_to_all(slab, axis, split_axis=0, concat_axis=0, tiled=True)  25.1 us
    unnamed x11, local copies, waits for them, and re-layouts  8.96 us
  transfers between devices with their start and end apart: 3, of which 2 were waited for; matrix products, arithmetic and copies ran while one was open for 6% of the time, Pallas kernels for 0%

commit v1 on v0

--- a/solution.py
+++ b/solution.py
@@ -51,7 +51,7 @@
 
 def over_axes(array, axes):
     for axis in axes:
-        array = lax.psum(array, axis)
+        array = jnp.sum(lax.all_gather(array, axis), 0)
     return array
 
 

time: 302 us -> 337 us (1.12)
  blocking collectives: 92.1 us -> 124 us
  local copies, waits for them, and re-layouts: 19.4 us -> 28.9 us
  waiting for transfers between devices: 135 us -> 126 us
    unnamed x0 -> x5, blocking collectives: none -> 85.3 us
    psum x5 -> x0, blocking collectives: 53.4 us -> none  [over_axes(): array = lax.psum(array, axis)]
    all_to_all x2, waiting for transfers between devices: 135 us -> 126 us  [several_exchanges(): lax.all_to_all(slab, axis, split_axis=0, concat_axis=0, tiled=True)]
    unnamed x11 -> x36, local copies, waits for them, and re-layouts: 8.96 us -> 17.7 us
  transfers between devices with their start and end apart: 3 -> 3, of which waited for: 2 -> 2; matrix products, arithmetic and copies ran while one was open for 6% -> 7% of each run, Pallas kernels for 0% -> 0%
where the time goes in v1:
time: 337 us
  waiting for transfers between devices  126 us (37%)
  blocking collectives  124 us (37%)
  local copies, waits for them, and re-layouts  28.9 us (9%)
  starting transfers between devices  25.2 us (7%)
  between operations  17.5 us (5%)
  other arithmetic  11.5 us (3%)
  matrix products  4.32 us (1%)
    all_to_all x2, waiting for transfers between devices, several_exchanges(): lax.all_to_all(slab, axis, split_axis=0, concat_axis=0, tiled=True)  126 us
    unnamed x5, blocking collectives  85.3 us
    psum x1, blocking collectives, body(): embed_cols = lax.psum(found.astype(jnp.bfloat16), GROUP).astype(jnp.float32)  38.6 us
    all_to_all x2, starting transfers between devices, several_exchanges(): lax.all_to_all(slab, axis, split_axis=0, concat_axis=0, tiled=True)  25.1 us
    unnamed x36, local copies, waits for them, and re-layouts  17.7 us
  transfers between devices with their start and end apart: 3, of which 2 were waited for; matrix products, arithmetic and copies ran while one was open for 7% of the time, Pallas kernels for 0%

profile of v1, /device:TPU:1, one launch (start us, length us, event | category | flops | bytes accessed | tf_op | source)
XLA Modules:
  0.0 336.7 jit_solution(7143466322642679538)
XLA Ops:
  7.2 2.8 copy.27
  9.9 0.0 copy-start.3
  9.9 0.2 split.8
  10.1 2.1 copy.24
  12.2 18.3 %all-to-all-start = ((bf16[64,32,384]{2,1,0:T(8,128)(2,1)}), bf16[64,32,384]{2,1,0:T(8,128)(2,1)}, u32[]{:S(2)}, u32[]{:S(2)}) async-start(bf16[64,32,384]{2,1,0:T(8,128)(2,1)} %copy.24), calls=%async_computation | async-start | bytes 3145728 | tf_op jit(solution)/shard_map/all_to_all | solution.py:48
  30.5 0.0 all-gather.12.cloned.1.call-start
  30.5 0.0 copy-done.3
  30.6 0.7 copy.23
  31.3 1.6 pad_maximum_fusion.1
  32.9 0.0 all-gather.12.cloned.1.call-update
  32.9 0.2 split.9
  33.1 0.0 copy-start
  33.1 2.4 copy.25
  35.6 79.7 %all-to-all-done = bf16[64,32,384]{2,1,0:T(8,128)(2,1)} async-done(((bf16[64,32,384]{2,1,0:T(8,128)(2,1)}), bf16[64,32,384]{2,1,0:T(8,128)(2,1)}, u32[]{:S(2)}, u32[]{:S(2)}) %all-to-all-start) | async-done | bytes 1572896 | tf_op jit(solution)/shard_map/all_to_all | solution.py:48
  115.3 6.8 %all-to-all-start.1 = ((bf16[64,40,384]{2,1,0:T(8,128)(2,1)}), bf16[64,40,384]{2,1,0:T(8,128)(2,1)}, u32[]{:S(2)}, u32[]{:S(2)}) async-start(bf16[64,40,384]{2,1,0:T(8,128)(2,1)} %copy.25), calls=%async_computation.1 | async-start | bytes 3932160 | tf_op jit(solution)/shard_map/all_to_all | solution.py:48
  122.1 0.0 copy-done
  122.1 0.0 copy-start.2
  122.1 5.3 %copy.22 = bf16[72,24576]{0,1:T(8,128)(2,1)} copy(bf16[72,24576]{1,0:T(8,128)(2,1)S(1)} %copy-done) | data formatting | bytes 7077888 | tf_op args[0]
  127.4 1.3 dynamic-slice
  128.6 1.3 dynamic-slice.1
  131.2 1.3 dynamic-slice.2
  133.1 1.3 dynamic-slice.3
  135.1 1.3 dynamic-slice.4
  137.0 0.0 copy-done.2
  137.0 4.8 %gather_fusion = bf16[448,72]{1,0:T(8,128)(2,1)S(1)} fusion(bf16[72,24576]{0,1:T(8,128)(2,1)} %copy.22, s32[1024]{0:T(1024)S(1)} %pad_clamp_fusion), kind=kCustom, calls=%fused_computation | custom fusion | bytes 130816 | tf_op jit(solution)/shard_map/jit(_take)/gather | solution.py:67
  141.9 0.2 multiply_convert_fusion
  142.0 38.6 %psum.7 = bf16[448,72]{1,0:T(8,128)(2,1)S(1)} all-reduce(bf16[448,72]{1,0:T(8,128)(2,1)S(1)} %multiply_convert_fusion), channel_id=1, replica_groups=mesh['group_0'=4,'group_1'=2,'vocab_0'=16,'vocab_1'=2,'vocab_2'=2] {'gro..., use_global_device_ids=true, to_apply=%region_0.1 | all-reduce | flops 32256 | bytes 129024 | tf_op jit(solution)/shard_map/psum | solution.py:69
  180.7 0.7 copy.26
  181.4 45.9 %all-to-all-done.1 = bf16[64,40,384]{2,1,0:T(8,128)(2,1)} async-done(((bf16[64,40,384]{2,1,0:T(8,128)(2,1)}), bf16[64,40,384]{2,1,0:T(8,128)(2,1)}, u32[]{:S(2)}, u32[]{:S(2)}) %all-to-all-start.1) | async-done | bytes 1966112 | tf_op jit(solution)/shard_map/all_to_all | solution.py:48
  227.3 2.4 pad_maximum_fusion
  229.6 0.0 all-gather.12.cloned.1.call-done
  229.7 0.0 copy-start.1
  229.7 3.6 %fusion.2 = f32[448]{0:T(512)S(1)} fusion(bf16[4608,449]{1,0:T(8,128)(2,1)} %all-gather.12.cloned.1.call-done), kind=kLoop, calls=%fused_computation.5 | loop fusion | flops 6192704 | bytes 4130560 | tf_op jit(solution)/shard_map/reduce_sum | solution.py:73
  233.2 0.2 copy-done.1
  233.4 0.8 convert_reduce_fusion
  234.2 4.3 %select_reduce_fusion = (f32[448]{0:T(512)S(1)}, f32[448]{0:T(512)S(1)}, f32[448,384]{1,0:T(8,128)}) fusion(s32[448]{0:T(512)S(1)} %broadcast_subtract_fusion.1, bf16[4608,384]{1,0:T(8,128)(2,1)S(1)} %bitcast.16, f32[448]{0:T(512)S(1)} %add_rsqrt_fusion, f32[4608]{0:T(1024)S(1)} %convert_reduce_fusion, bf16[4608,449]{1,0:T(8,128)(2,1)S(1)} %copy-done.1), kind=kOutput, calls=%fused_computation.15 | convolution fusion | flops 1594735616 | bytes 8390656 | tf_op jit(solution)/shard_map/dot_general | solution.py:78
  238.6 0.2 dynamic-update-slice
  238.8 0.3 dynamic-update-slice.5
  239.0 12.9 %all-reduce.11 = (f32[1792]{0:T(1024)S(1)}, f32[1792]{0:T(1024)S(1)}) all-reduce(f32[1792]{0:T(1024)S(1)} %dynamic-update-slice, f32[1792]{0:T(1024)S(1)} %dynamic-update-slice.5), channel_id=2, replica_groups=mesh['group_0'=4,'group_1'=2,'vocab_0'=16,'vocab_1'=2,'vocab_2'=2] {'gro..., use_global_device_ids=true, to_apply=%add | all-reduce | flops 3584 | bytes 28672
  251.9 0.1 reshape.59
  251.9 0.1 reshape.54
  252.1 0.2 dynamic-update-slice.6
  252.3 0.2 dynamic-update-slice.1
  252.5 5.3 %all-reduce.14 = (f32[896]{0:T(1024)S(1)}, f32[896]{0:T(1024)S(1)}) all-reduce(f32[896]{0:T(1024)S(1)} %dynamic-update-slice.1, f32[896]{0:T(1024)S(1)} %dynamic-update-slice.6), channel_id=3, replica_groups=mesh['group_0'=4,'group_1'=2,'vocab_0'=16,'vocab_1'=2,'vocab_2'=2] {'gro..., use_global_device_ids=true, to_apply=%add.1 | all-reduce | flops 1792 | bytes 14336
  257.8 0.1 reshape.60
  257.9 0.1 reshape.55
  258.1 0.3 dynamic-update-slice.7
  258.3 0.3 dynamic-update-slice.2
  258.6 41.0 %all-reduce.10 = (f32[7168]{0:T(1024)S(1)}, f32[7168]{0:T(1024)S(1)}) all-reduce(f32[7168]{0:T(1024)S(1)} %dynamic-update-slice.2, f32[7168]{0:T(1024)S(1)} %dynamic-update-slice.7), channel_id=4, replica_groups=mesh['group_0'=4,'group_1'=2,'vocab_0'=16,'vocab_1'=2,'vocab_2'=2] {'voc..., use_global_device_ids=true, to_apply=%add.2 | all-reduce | flops 14336 | bytes 114688
  299.6 0.1 reshape.61
  299.7 0.1 reshape.56
  299.8 0.2 dynamic-update-slice.8
  300.0 0.2 dynamic-update-slice.3
  300.3 3.8 %all-reduce.13 = (f32[896]{0:T(1024)S(1)}, f32[896]{0:T(1024)S(1)}) all-reduce(f32[896]{0:T(1024)S(1)} %dynamic-update-slice.3, f32[896]{0:T(1024)S(1)} %dynamic-update-slice.8), channel_id=5, replica_groups=mesh['group_0'=4,'group_1'=2,'vocab_0'=16,'vocab_1'=2,'vocab_2'=2] {'voc..., use_global_device_ids=true, to_apply=%add.3 | all-reduce | flops 1792 | bytes 14336
  304.1 0.1 reshape.62
  304.1 0.1 reshape.57
  304.3 0.2 dynamic-update-slice.9
  304.5 0.2 dynamic-update-slice.4
  304.7 22.3 %all-reduce.12 = (f32[896]{0:T(1024)S(1)}, f32[896]{0:T(1024)S(1)}) all-reduce(f32[896]{0:T(1024)S(1)} %dynamic-update-slice.4, f32[896]{0:T(1024)S(1)} %dynamic-update-slice.9), channel_id=6, replica_groups=mesh['group_0'=4,'group_1'=2,'vocab_0'=16,'vocab_1'=2,'vocab_2'=2] {'voc..., use_global_device_ids=true, to_apply=%add.4 | all-reduce | flops 1792 | bytes 14336
  327.0 0.1 reshape.58
  327.1 0.1 reshape.63
  327.2 0.6 log_subtract_fusion
  327.8 2.1 broadcast_subtract_fusion
  (25 shorter events, 0.3 us)
Async XLA Ops:
  9.9 20.6 %copy-start.3 = (bf16[72]{0:T(256)(128)(2,1)S(1)}, bf16[72]{0:T(256)(128)(2,1)}, u32[]{:S(2)}) copy-start(bf16[72]{0:T(256)(128)(2,1)} %param.6) | copy-start | bytes 436
  12.2 103.1 %all-to-all-start = ((bf16[64,32,384]{2,1,0:T(8,128)(2,1)}), bf16[64,32,384]{2,1,0:T(8,128)(2,1)}, u32[]{:S(2)}, u32[]{:S(2)}) async-start(bf16[64,32,384]{2,1,0:T(8,128)(2,1)} %copy.24), calls=%async_computation | async-start | bytes 3145728 | tf_op jit(solution)/shard_map/all_to_all | solution.py:48
  30.5 199.1 %all-gather.12.cloned.1.call-start = ((), (), s32[]{:S(2)}) async-start(), calls=%async_computation.2 | async-start | bytes 4792320 | tf_op jit(solution)/shard_map/all_gather | solution.py:16
  33.1 89.0 %copy-start = (bf16[72,24576]{1,0:T(8,128)(2,1)S(1)}, bf16[72,24576]{1,0:T(8,128)(2,1)}, u32[]{:S(2)}) copy-start(bf16[72,24576]{1,0:T(8,128)(2,1)} %param.4) | copy-start | bytes 10616836
  115.3 112.0 %all-to-all-start.1 = ((bf16[64,40,384]{2,1,0:T(8,128)(2,1)}), bf16[64,40,384]{2,1,0:T(8,128)(2,1)}, u32[]{:S(2)}, u32[]{:S(2)}) async-start(bf16[64,40,384]{2,1,0:T(8,128)(2,1)} %copy.25), calls=%async_computation.1 | async-start | bytes 3932160 | tf_op jit(solution)/shard_map/all_to_all | solution.py:48
  122.1 14.9 %copy-start.2 = (s32[448]{0:T(512)S(1)}, s32[448]{0:T(512)}, u32[]{:S(2)}) copy-start(s32[448]{0:T(512)} %param.7) | copy-start | bytes 5380
  229.7 3.8 %copy-start.1 = (bf16[4608,449]{1,0:T(8,128)(2,1)S(1)}, bf16[4608,449]{1,0:T(8,128)(2,1)}, u32[]{:S(2)}) copy-start(bf16[4608,449]{1,0:T(8,128)(2,1)} %all-gather.12.cloned.1.call-done) | copy-start | bytes 12413956
Sparse Core Ops, SparseCore 0:
  34.0 191.6 all-gather.11
